TPU v7x, 8 devices: a whole 2x2x1 slice. The times are simulated.
8 devices in a mesh: seqs: 1 (over z), rows: 2 (over y), states: 4 (over x, core).
Axes of the slice: x: 2, y: 2, z: 1, core: 2. Of those that a mesh axis runs over, the one named last changes fastest.
Arguments:
- trans_mat: bfloat16 [16384, 2, 8192], P('rows', None, 'states')
- emit_mat: bfloat16 [16384, 10000], P(('rows', 'states'))
- init_dist: float32 [16384], P(('rows', 'states'))
- tokens: int32 [64, 32], P('seqs')
- lengths: int32 [64], P('seqs')
Outputs:
- output 1: float32 [64], P('seqs')
- output 2: float32 [64, 16384], P('seqs', ('rows', 'states'))
All inputs are finite; a program needn't handle non-finite values.
Results may differ from a plain program's by a relative error of at most 0.001.
Values are sent between devices in bfloat16 or wider.
A program may use at most 1 GiB of HBM per device.

v0:
```python
import jax
import jax.numpy as jnp
from jax import lax
from jax.sharding import PartitionSpec as P


def solution(mesh):
    vec_axes = ('rows', 'states')

    def local_forward(trans_blk, emit_blk, init_blk, tokens, lengths):
        n_steps = tokens.shape[1]
        emis_all = jnp.transpose(jnp.take(emit_blk, tokens, axis=1), (2, 1, 0))
        first_raw = init_blk[None, :] * emis_all[0].astype(jnp.float32)
        norm_c = lax.psum(jnp.sum(first_raw, axis=1), vec_axes)
        alpha_init = first_raw / norm_c[:, None]
        loglik_init = jnp.log(norm_c)

        def one_step(state_in, inputs):
            alpha_cur, loglik = state_in
            emis_t, t_index = inputs
            gathered = lax.all_gather(alpha_cur.astype(jnp.bfloat16), 'states', axis=1, tiled=True)
            part_sum = jnp.einsum('bk,kaq->baq', gathered, trans_blk, preferred_element_type=jnp.float32)
            mix_sum = lax.psum_scatter(part_sum, 'rows', scatter_dimension=1, tiled=True)[:, 0, :]
            raw_next = mix_sum * emis_t.astype(jnp.float32)
            norm_step = lax.psum(jnp.sum(raw_next, axis=1), vec_axes)
            active = t_index < lengths
            alpha_cur = jnp.where(active[:, None], raw_next / norm_step[:, None], alpha_cur)
            loglik = loglik + jnp.where(active, jnp.log(norm_step), 0.0)
            return (alpha_cur, loglik), None

        scan_out = lax.scan(one_step, (alpha_init, loglik_init), (emis_all[1:], jnp.arange(1, n_steps)))
        alpha_last, loglik = scan_out[0]
        return loglik, alpha_last

    return jax.shard_map(local_forward, mesh=mesh, in_specs=(P('rows', None, 'states'), P(vec_axes, None), P(vec_axes), P('seqs', None), P('seqs')), out_specs=(P('seqs'), P('seqs', vec_axes)), check_vma=False)
```

profile of v0, /device:TPU:0, one launch (start us, length us, event | category | flops | bytes accessed | tf_op | source)
XLA Modules:
  0.0 2866.4 jit_solution(13594854144492737666)
XLA Ops:
  8.1 48.1 %gather_fusion = bf16[2048,2048]{1,0:T(8,128)(2,1)} fusion(bf16[2048,10000]{0,1:T(8,128)(2,1)} %param.8, s32[2048]{0:T(1024)S(1)} %broadcast_clamp_fusion), kind=kCustom, calls=%fused_computation | custom fusion | bytes 16785408 | tf_op jit(solution)/shard_map/jit(_take)/gather | solution.py:12
  75.7 25.3 psum.14
  110.1 44.2 %copy.11 = bf16[8192,2,2048]{2,0,1:T(8,128)(2,1)} copy(bf16[8192,2,2048]{2,1,0:T(2,128)(2,1)} %param.7) | data formatting | bytes 134217728 | tf_op jit(solution)/shard_map/while | solution.py:31
  154.4 2704.7 %while.12 = (s32[]{:T(128)}, f32[64,2048]{1,0:T(8,128)S(1)}, f32[64]{0:T(128)S(1)}, s32[31]{0:T(128)S(1)}, s32[64]{0:T(128)S(1)}, /*index=5*/bf16[8192,2,2048]{2...) while((s32[]{:T(128)}, f32[64,2048]{1,0:T(8,128)S(1)}, f32[64]{0:T(128)S(1)}, s32[31]{0:T(128)S(1)}, ...), condition=%wide.region_6.7_spmd, body=%wide.region_2.6_spmd.sunk | while | flops 4296015872 | bytes 81267016 | solution.py:31
  171.8 25.9 fusion.12
  216.7 22.3 psum.16
  259.3 25.9 fusion.12
  304.1 22.3 psum.16
  346.4 25.9 fusion.12
  433.8 25.9 fusion.12
  478.6 22.3 psum.16
  521.2 25.9 fusion.12
  566.1 22.3 psum.16
  608.6 25.9 fusion.12
  653.5 22.3 psum.16
  696.0 25.9 fusion.12
  740.9 22.3 psum.16
  783.1 25.9 fusion.12
  828.0 22.3 psum.16
  870.3 25.9 fusion.12
  957.7 25.9 fusion.12
  1002.5 22.3 psum.16
  1045.1 25.9 fusion.12
  1090.0 22.3 psum.16
  1132.5 25.9 fusion.12
  1177.4 22.3 psum.16
  1219.9 25.9 fusion.12
  1264.8 22.3 psum.16
  1307.0 25.9 fusion.12
  1351.9 22.3 psum.16
  1394.5 25.9 fusion.12
  1439.3 22.3 psum.16
  1481.9 25.9 fusion.12
  1569.0 25.9 fusion.12
  1656.4 25.9 fusion.12
  1743.5 25.9 fusion.12
  1830.6 25.9 fusion.12
  1918.0 25.9 fusion.12
  2005.1 25.9 fusion.12
  2092.2 25.9 fusion.12
  2179.3 25.9 fusion.12
  2266.4 25.9 fusion.12
  2353.6 25.9 fusion.12
  2440.7 25.9 fusion.12
  2528.1 25.9 fusion.12
  2615.5 25.9 fusion.12
  2702.6 25.9 fusion.12
  2790.0 25.9 fusion.12
  (382 shorter events, 1641.3 us)
Async XLA Ops:
  155.2 60.3 %reduce-scatter.2.cloned.1.call-start = ((), (), s32[]{:S(2)}) async-start(), calls=%async_computation.2 | async-start | bytes 1572864 | tf_op jit(solution)/shard_map/while/body/eval_jaxpr/reduce_scatter | solution.py:23
  240.9 18.4 all-gather.2.cloned.1.call-start
  241.7 61.2 %reduce-scatter.2.cloned.1.call-start = ((), (), s32[]{:S(2)}) async-start(), calls=%async_computation.2 | async-start | bytes 1572864 | tf_op jit(solution)/shard_map/while/body/eval_jaxpr/reduce_scatter | solution.py:23
  328.3 18.1 all-gather.2.cloned.1.call-start
  329.1 60.8 %reduce-scatter.2.cloned.1.call-start = ((), (), s32[]{:S(2)}) async-start(), calls=%async_computation.2 | async-start | bytes 1572864 | tf_op jit(solution)/shard_map/while/body/eval_jaxpr/reduce_scatter | solution.py:23
  415.4 18.4 all-gather.2.cloned.1.call-start
  416.2 61.2 %reduce-scatter.2.cloned.1.call-start = ((), (), s32[]{:S(2)}) async-start(), calls=%async_computation.2 | async-start | bytes 1572864 | tf_op jit(solution)/shard_map/while/body/eval_jaxpr/reduce_scatter | solution.py:23
  502.8 18.4 all-gather.2.cloned.1.call-start
  503.6 61.2 %reduce-scatter.2.cloned.1.call-start = ((), (), s32[]{:S(2)}) async-start(), calls=%async_computation.2 | async-start | bytes 1572864 | tf_op jit(solution)/shard_map/while/body/eval_jaxpr/reduce_scatter | solution.py:23
  590.2 18.4 all-gather.2.cloned.1.call-start
  591.1 61.2 %reduce-scatter.2.cloned.1.call-start = ((), (), s32[]{:S(2)}) async-start(), calls=%async_computation.2 | async-start | bytes 1572864 | tf_op jit(solution)/shard_map/while/body/eval_jaxpr/reduce_scatter | solution.py:23
  677.7 18.4 all-gather.2.cloned.1.call-start
  678.5 61.2 %reduce-scatter.2.cloned.1.call-start = ((), (), s32[]{:S(2)}) async-start(), calls=%async_computation.2 | async-start | bytes 1572864 | tf_op jit(solution)/shard_map/while/body/eval_jaxpr/reduce_scatter | solution.py:23
  765.9 60.8 %reduce-scatter.2.cloned.1.call-start = ((), (), s32[]{:S(2)}) async-start(), calls=%async_computation.2 | async-start | bytes 1572864 | tf_op jit(solution)/shard_map/while/body/eval_jaxpr/reduce_scatter | solution.py:23
  853.0 60.8 %reduce-scatter.2.cloned.1.call-start = ((), (), s32[]{:S(2)}) async-start(), calls=%async_computation.2 | async-start | bytes 1572864 | tf_op jit(solution)/shard_map/while/body/eval_jaxpr/reduce_scatter | solution.py:23
  939.3 18.4 all-gather.2.cloned.1.call-start
  940.1 61.2 %reduce-scatter.2.cloned.1.call-start = ((), (), s32[]{:S(2)}) async-start(), calls=%async_computation.2 | async-start | bytes 1572864 | tf_op jit(solution)/shard_map/while/body/eval_jaxpr/reduce_scatter | solution.py:23
  1026.7 18.4 all-gather.2.cloned.1.call-start
  1027.5 61.2 %reduce-scatter.2.cloned.1.call-start = ((), (), s32[]{:S(2)}) async-start(), calls=%async_computation.2 | async-start | bytes 1572864 | tf_op jit(solution)/shard_map/while/body/eval_jaxpr/reduce_scatter | solution.py:23
  1114.1 18.4 all-gather.2.cloned.1.call-start
  1114.9 61.2 %reduce-scatter.2.cloned.1.call-start = ((), (), s32[]{:S(2)}) async-start(), calls=%async_computation.2 | async-start | bytes 1572864 | tf_op jit(solution)/shard_map/while/body/eval_jaxpr/reduce_scatter | solution.py:23
  1201.6 18.4 all-gather.2.cloned.1.call-start
  1202.4 61.2 %reduce-scatter.2.cloned.1.call-start = ((), (), s32[]{:S(2)}) async-start(), calls=%async_computation.2 | async-start | bytes 1572864 | tf_op jit(solution)/shard_map/while/body/eval_jaxpr/reduce_scatter | solution.py:23
  1289.8 60.8 %reduce-scatter.2.cloned.1.call-start = ((), (), s32[]{:S(2)}) async-start(), calls=%async_computation.2 | async-start | bytes 1572864 | tf_op jit(solution)/shard_map/while/body/eval_jaxpr/reduce_scatter | solution.py:23
  1376.1 18.4 all-gather.2.cloned.1.call-start
  1376.9 61.2 %reduce-scatter.2.cloned.1.call-start = ((), (), s32[]{:S(2)}) async-start(), calls=%async_computation.2 | async-start | bytes 1572864 | tf_op jit(solution)/shard_map/while/body/eval_jaxpr/reduce_scatter | solution.py:23
  1463.5 18.4 all-gather.2.cloned.1.call-start
  1464.3 61.2 %reduce-scatter.2.cloned.1.call-start = ((), (), s32[]{:S(2)}) async-start(), calls=%async_computation.2 | async-start | bytes 1572864 | tf_op jit(solution)/shard_map/while/body/eval_jaxpr/reduce_scatter | solution.py:23
  1551.7 60.8 %reduce-scatter.2.cloned.1.call-start = ((), (), s32[]{:S(2)}) async-start(), calls=%async_computation.2 | async-start | bytes 1572864 | tf_op jit(solution)/shard_map/while/body/eval_jaxpr/reduce_scatter | solution.py:23
  1638.0 18.4 all-gather.2.cloned.1.call-start
  1638.8 61.2 %reduce-scatter.2.cloned.1.call-start = ((), (), s32[]{:S(2)}) async-start(), calls=%async_computation.2 | async-start | bytes 1572864 | tf_op jit(solution)/shard_map/while/body/eval_jaxpr/reduce_scatter | solution.py:23
  1726.2 60.8 %reduce-scatter.2.cloned.1.call-start = ((), (), s32[]{:S(2)}) async-start(), calls=%async_computation.2 | async-start | bytes 1572864 | tf_op jit(solution)/shard_map/while/body/eval_jaxpr/reduce_scatter | solution.py:23
  1813.4 60.8 %reduce-scatter.2.cloned.1.call-start = ((), (), s32[]{:S(2)}) async-start(), calls=%async_computation.2 | async-start | bytes 1572864 | tf_op jit(solution)/shard_map/while/body/eval_jaxpr/reduce_scatter | solution.py:23
  1899.6 18.4 all-gather.2.cloned.1.call-start
  1900.5 61.2 %reduce-scatter.2.cloned.1.call-start = ((), (), s32[]{:S(2)}) async-start(), calls=%async_computation.2 | async-start | bytes 1572864 | tf_op jit(solution)/shard_map/while/body/eval_jaxpr/reduce_scatter | solution.py:23
  1987.9 60.8 %reduce-scatter.2.cloned.1.call-start = ((), (), s32[]{:S(2)}) async-start(), calls=%async_computation.2 | async-start | bytes 1572864 | tf_op jit(solution)/shard_map/while/body/eval_jaxpr/reduce_scatter | solution.py:23
  2075.0 60.8 %reduce-scatter.2.cloned.1.call-start = ((), (), s32[]{:S(2)}) async-start(), calls=%async_computation.2 | async-start | bytes 1572864 | tf_op jit(solution)/shard_map/while/body/eval_jaxpr/reduce_scatter | solution.py:23
  2162.1 60.8 %reduce-scatter.2.cloned.1.call-start = ((), (), s32[]{:S(2)}) async-start(), calls=%async_computation.2 | async-start | bytes 1572864 | tf_op jit(solution)/shard_map/while/body/eval_jaxpr/reduce_scatter | solution.py:23
  2249.2 60.8 %reduce-scatter.2.cloned.1.call-start = ((), (), s32[]{:S(2)}) async-start(), calls=%async_computation.2 | async-start | bytes 1572864 | tf_op jit(solution)/shard_map/while/body/eval_jaxpr/reduce_scatter | solution.py:23
  2336.3 60.8 %reduce-scatter.2.cloned.1.call-start = ((), (), s32[]{:S(2)}) async-start(), calls=%async_computation.2 | async-start | bytes 1572864 | tf_op jit(solution)/shard_map/while/body/eval_jaxpr/reduce_scatter | solution.py:23
  2423.4 60.8 %reduce-scatter.2.cloned.1.call-start = ((), (), s32[]{:S(2)}) async-start(), calls=%async_computation.2 | async-start | bytes 1572864 | tf_op jit(solution)/shard_map/while/body/eval_jaxpr/reduce_scatter | solution.py:23
  2509.7 18.4 all-gather.2.cloned.1.call-start
  2510.5 61.2 %reduce-scatter.2.cloned.1.call-start = ((), (), s32[]{:S(2)}) async-start(), calls=%async_computation.2 | async-start | bytes 1572864 | tf_op jit(solution)/shard_map/while/body/eval_jaxpr/reduce_scatter | solution.py:23
  2597.1 18.4 all-gather.2.cloned.1.call-start
  2597.9 61.2 %reduce-scatter.2.cloned.1.call-start = ((), (), s32[]{:S(2)}) async-start(), calls=%async_computation.2 | async-start | bytes 1572864 | tf_op jit(solution)/shard_map/while/body/eval_jaxpr/reduce_scatter | solution.py:23
  2685.3 60.8 %reduce-scatter.2.cloned.1.call-start = ((), (), s32[]{:S(2)}) async-start(), calls=%async_computation.2 | async-start | bytes 1572864 | tf_op jit(solution)/shard_map/while/body/eval_jaxpr/reduce_scatter | solution.py:23
  2771.6 18.4 all-gather.2.cloned.1.call-start
  2772.5 61.2 %reduce-scatter.2.cloned.1.call-start = ((), (), s32[]{:S(2)}) async-start(), calls=%async_computation.2 | async-start | bytes 1572864 | tf_op jit(solution)/shard_map/while/body/eval_jaxpr/reduce_scatter | solution.py:23
  (20 other events, 368.8 us)
Sparse Core Ops, SparseCore 0:
  197.9 17.5 reduce-scatter.1
  285.3 17.5 reduce-scatter.1
  330.9 15.4 all-gather.1
  372.4 17.5 reduce-scatter.1
  418.3 15.4 all-gather.1
  459.8 17.5 reduce-scatter.1
  505.7 15.4 all-gather.1
  547.2 17.5 reduce-scatter.1
  593.2 15.4 all-gather.1
  634.7 17.5 reduce-scatter.1
  680.6 15.4 all-gather.1
  722.1 17.5 reduce-scatter.1
  809.2 17.5 reduce-scatter.1
  896.3 17.5 reduce-scatter.1
  942.2 15.4 all-gather.1
  983.7 17.5 reduce-scatter.1
  1029.6 15.4 all-gather.1
  1071.1 17.5 reduce-scatter.1
  1158.5 17.5 reduce-scatter.1
  1204.5 15.4 all-gather.1
  1246.0 17.5 reduce-scatter.1
  1333.1 17.5 reduce-scatter.1
  1420.5 17.5 reduce-scatter.1
  1466.4 15.4 all-gather.1
  1507.9 17.5 reduce-scatter.1
  1595.0 17.5 reduce-scatter.1
  1640.9 15.4 all-gather.1
  1682.4 17.5 reduce-scatter.1
  1728.0 15.4 all-gather.1
  1769.5 17.5 reduce-scatter.1
  1815.1 15.4 all-gather.1
  1856.6 17.5 reduce-scatter.1
  1902.6 15.4 all-gather.1
  1944.1 17.5 reduce-scatter.1
  2031.2 17.5 reduce-scatter.1
  2118.3 17.5 reduce-scatter.1
  2163.9 15.4 all-gather.1
  2205.4 17.5 reduce-scatter.1
  2251.0 15.4 all-gather.1
  2292.5 17.5 reduce-scatter.1
  2379.6 17.5 reduce-scatter.1
  2466.7 17.5 reduce-scatter.1
  2554.1 17.5 reduce-scatter.1
  2641.5 17.5 reduce-scatter.1
  2687.1 15.4 all-gather.1
  2728.6 17.5 reduce-scatter.1
  2774.6 15.4 all-gather.1
  2816.1 17.5 reduce-scatter.1
  (14 shorter events, 214.1 us)
where the time goes:
time: 2870 us
  waiting for transfers between devices  1070 us (37%)
  matrix products  803 us (28%)
  blocking collectives  715 us (25%)
  other arithmetic  139 us (5%)
  local copies, waits for them, and re-layouts  123 us (4%)
    dot_general x31, matrix products, one_step(): jnp.einsum('bk,kaq->baq', gathered, trans_blk, preferred_element_type=jnp...  803 us
    psum x31, blocking collectives, one_step(): norm_step = lax.psum(jnp.sum(raw_next, axis=1), vec_axes)  690 us
    all_gather x31, waiting for transfers between devices, one_step(): lax.all_gather(alpha_cur.astype(jnp.bfloat16), 'states', axis=1, tiled=True)  538 us
    reduce_scatter x31, waiting for transfers between devices, one_step(): lax.psum_scatter(part_sum, 'rows', scatter_dimension=1, tiled=True)[:, 0, :]  530 us
  transfers between devices with their start and end apart: 62, of which 62 were waited for; matrix products, arithmetic and copies ran while one was open for 1% of the time, Pallas kernels for 0%

commit v1 on v0

v1 whole, which is shorter than its diff:
```python
import functools

import jax
import jax.numpy as jnp
from jax import lax
from jax.experimental import pallas as pl
from jax.experimental.pallas import tpu as pltpu
from jax.sharding import PartitionSpec as P

MESH = pl.DeviceIdType.MESH
LANES = 128
GROUP = 8


def forward_kernel(
    n_steps, rows, width, piece, chunk, depth,
    a_hbm, emis_hbm, init_ref, len_pack, len_col,
    ll_ref, alpha_ref,
    held, ring, a_bf, gath, y_out, y_in, emis, c_buf, c_acc, inv_b,
    held_sem, ring_sem, emis_sem, y_ss, y_rs, x_ss, x_rs, p_ss, p_rs, f_ss, f_rs, c_ss, c_rs,
    credit_x, credit_p,
):
    n_pieces = width // piece
    n_chunks = width // chunk
    n_held_own = held.shape[0] - n_chunks
    per_chunk = chunk // piece
    k_parts = a_bf.shape[1] // depth
    row = lax.axis_index('rows')
    st = lax.axis_index('states')
    across = lax.rem(st + 2, 4)
    partner = st + 1 - 2 * lax.rem(st, 2)
    other = 1 - row
    me = row * 4 + st
    to_y = {'rows': other}
    to_x = {'states': across}
    to_p = {'states': partner}
    peers = []
    for k in range(1, 8):
        peers.append({'rows': lax.rem(row + k // 4, 2), 'states': lax.rem(st + k % 4, 4)})

    barrier = pltpu.get_barrier_semaphore()
    for peer in peers:
        pl.semaphore_signal(barrier, inc=1, device_id=peer, device_id_type=MESH)

    def held_copy(ch):
        half, c = (other, ch) if ch < n_chunks else (row, ch - n_chunks)
        return pltpu.make_async_copy(a_hbm.at[half, :, pl.ds(c * chunk, chunk)], held.at[ch], held_sem.at[ch])

    def ring_copy(c, k):
        cols = pl.ds(pl.multiple_of(c * chunk, chunk), chunk)
        return pltpu.make_async_copy(a_hbm.at[row, pl.ds(k * depth, depth), cols], ring.at[k], ring_sem.at[k])

    def emis_copy(t, slot):
        return pltpu.make_async_copy(emis_hbm.at[t, pl.ds(0, rows)], emis.at[slot], emis_sem.at[slot])

    def remote(src, dst, ss, rs, dev):
        return pltpu.make_async_remote_copy(src_ref=src, dst_ref=dst, send_sem=ss, recv_sem=rs, device_id=dev, device_id_type=MESH)

    def y_copy(p):
        return remote(y_out.at[p], y_in.at[p], y_ss.at[p], y_rs.at[p], to_y)

    def x_copy(p):
        return remote(gath.at[st, p], gath.at[st, p], x_ss.at[p], x_rs.at[p], to_x)

    def x_arrived(p):
        return remote(gath.at[across, p], gath.at[across, p], x_ss.at[p], x_rs.at[p], to_x)

    def p_copy(p):
        return remote(gath.at[st, p], gath.at[st, p], p_ss.at[p], p_rs.at[p], to_p)

    def p_arrived(p):
        return remote(gath.at[partner, p], gath.at[partner, p], p_ss.at[p], p_rs.at[p], to_p)

    def f_copy(p):
        return remote(gath.at[across, p], gath.at[across, p], f_ss.at[p], f_rs.at[p], to_p)

    def f_arrived(p):
        far = lax.rem(partner + 2, 4)
        return remote(gath.at[far, p], gath.at[far, p], f_ss.at[p], f_rs.at[p], to_p)

    def c_copy(par, k):
        return remote(c_buf.at[par, me], c_buf.at[par, me], c_ss.at[k], c_rs.at[par, k], peers[k - 1])

    def c_arrived(par, k):
        src = lax.rem(row + k // 4, 2) * 4 + lax.rem(st + 4 - k % 4, 4)
        return remote(c_buf.at[par, src], c_buf.at[par, src], c_ss.at[k], c_rs.at[par, k], peers[k - 1])

    emis_copy(0, 0).start()
    for ch in range(held.shape[0]):
        held_copy(ch).start()
    for k in range(k_parts):
        ring_copy(n_held_own, k).start()
    emis_copy(1, 1).start()
    pl.semaphore_wait(barrier, 7)

    lane = lax.broadcasted_iota(jnp.int32, (GROUP, LANES), 1)
    ll_ref[...] = jnp.zeros_like(ll_ref)
    alpha_ref[...] = jnp.zeros_like(alpha_ref)

    def emit_piece(p, value, cols, par):
        r = value * emis[par, :, cols].astype(jnp.float32)
        gath[st, p] = r
        part = r[:, :LANES]
        for j in range(1, piece // LANES):
            part = part + r[:, j * LANES:(j + 1) * LANES]
        c_acc[...] += part
        x_copy(p).start()
        p_copy(p).start()

    def forward(p):
        x_arrived(p).wait_recv()
        f_copy(p).start()

    def finish(t, first_forward):
        par = lax.rem(t, 2)
        pack = jnp.zeros((GROUP, LANES), jnp.float32)
        for i in range(rows // GROUP):
            total = jnp.sum(c_acc[pl.ds(i * GROUP, GROUP), :], axis=1, keepdims=True)
            pack = jnp.where(lane == i, total, pack)
        c_buf[par, me] = pack
        for k in range(1, 8):
            c_copy(par, k).start()
        c_acc[...] = jnp.zeros_like(c_acc)
        for p in range(first_forward, n_pieces):
            forward(p)
        for k in range(1, 8):
            c_arrived(par, k).wait_recv()
        total = c_buf[par, 0]
        for k in range(1, 8):
            total = total + c_buf[par, k]
        ll_ref[...] += jnp.where(t < len_pack[...], jnp.log(total), 0.0)
        inv = 1.0 / total
        for i in range(rows // GROUP):
            inv_b[pl.ds(i * GROUP, GROUP), :] = jnp.broadcast_to(inv[:, i:i + 1], (GROUP, LANES))

        def convert(src, p):
            scale = inv_b[...]
            for j in range(piece // LANES):
                at = pl.multiple_of(src * width + p * piece + j * LANES, LANES)
                a_bf[:, pl.ds(at, LANES)] = (gath[src, p, :, j * LANES:(j + 1) * LANES] * scale).astype(jnp.bfloat16)

        def convert_own(p, _):
            convert(st, p)
            convert(across, p)
            return 0

        lax.fori_loop(0, n_pieces, convert_own, 0)

        def convert_near(p, _):
            p_arrived(p).wait_recv()
            f_arrived(p).wait_recv()
            convert(partner, p)
            convert(lax.rem(partner + 2, 4), p)
            return 0

        lax.fori_loop(0, n_pieces, convert_near, 0)
        for p in range(n_pieces):
            x_copy(p).wait_send()
            p_copy(p).wait_send()
            f_copy(p).wait_send()
        for k in range(1, 8):
            c_copy(par, k).wait_send()

        @pl.when(t < n_steps - 1)
        def _():
            pl.semaphore_signal(credit_x, inc=1, device_id=to_x, device_id_type=MESH)
            pl.semaphore_signal(credit_p, inc=1, device_id=to_p, device_id_type=MESH)

        live = t < len_col[...]
        scale = inv_b[...]
        for p in range(n_pieces):
            for j in range(piece // LANES):
                cols = pl.ds(p * piece + j * LANES, LANES)
                alpha_ref[:, cols] = jnp.where(live, gath[st, p, :, j * LANES:(j + 1) * LANES] * scale, alpha_ref[:, cols])

    c_acc[...] = jnp.zeros_like(c_acc)
    emis_copy(0, 0).wait()
    for p in range(n_pieces):
        cols = pl.ds(p * piece, piece)
        emit_piece(p, jnp.broadcast_to(init_ref[:, cols], (rows, piece)), cols, 0)
    finish(0, 0)

    def one_step(t, _):
        par = lax.rem(t, 2)

        @pl.when(t + 1 < n_steps)
        def _():
            emis_copy(t + 1, 1 - par).start()

        def send_half(c, _):
            @pl.when(t == 1)
            def _():
                for ch in range(n_chunks):
                    @pl.when(c == ch)
                    def _():
                        held_copy(ch).wait()

            out = jnp.dot(a_bf[...], held[c], preferred_element_type=jnp.float32)
            for h in range(per_chunk):
                p = c * per_chunk + h
                y_out[p] = out[:, h * piece:(h + 1) * piece]
                y_copy(p).start()
            return 0

        lax.fori_loop(0, n_chunks, send_half, 0)
        pl.semaphore_wait(credit_x, 1)
        pl.semaphore_wait(credit_p, 1)
        emis_copy(t, par).wait()

        def pieces(c, out):
            for h in range(per_chunk):
                p = c * per_chunk + h
                y_copy(p).wait_recv()
                cols = pl.ds(pl.multiple_of(p * piece, piece), piece)
                emit_piece(p, out[:, h * piece:(h + 1) * piece] + y_in[p], cols, par)

            @pl.when(c > 0)
            def _():
                for h in range(per_chunk):
                    forward((c - 1) * per_chunk + h)

        def own_held(c, _):
            @pl.when(t == 1)
            def _():
                for ch in range(n_held_own):
                    @pl.when(c == ch)
                    def _():
                        held_copy(n_chunks + ch).wait()

            pieces(c, jnp.dot(a_bf[...], held[n_chunks + c], preferred_element_type=jnp.float32))
            return 0

        lax.fori_loop(0, n_held_own, own_held, 0)

        def own_streamed(c, _):
            out = None
            for k in range(k_parts):
                ring_copy(c, k).wait()
                term = jnp.dot(a_bf[:, k * depth:(k + 1) * depth], ring[k], preferred_element_type=jnp.float32)
                out = term if out is None else out + term
                last = c == n_chunks - 1

                @pl.when(jnp.logical_not(last))
                def _():
                    ring_copy(c + 1, k).start()

                @pl.when(jnp.logical_and(last, t < n_steps - 1))
                def _():
                    ring_copy(n_held_own, k).start()

            pieces(c, out)
            return 0

        lax.fori_loop(n_held_own, n_chunks, own_streamed, 0)
        for p in range(n_pieces):
            y_copy(p).wait_send()
        finish(t, n_pieces - per_chunk)
        return 0

    lax.fori_loop(1, n_steps, one_step, 0)


def run_forward(a_two, emis, init_row, len_pack, len_col, n_steps, rows, width):
    piece, chunk, depth, n_held = 256, 512, 2048, 6
    sources = a_two.shape[1]
    n_pieces = width // piece
    dma = pltpu.SemaphoreType.DMA
    any_spec = pl.BlockSpec(memory_space=pl.ANY)
    vmem = pl.BlockSpec(memory_space=pltpu.VMEM)
    return pl.pallas_call(
        functools.partial(forward_kernel, n_steps, rows, width, piece, chunk, depth),
        out_shape=(jax.ShapeDtypeStruct((GROUP, LANES), jnp.float32), jax.ShapeDtypeStruct((rows, width), jnp.float32)),
        in_specs=[any_spec, any_spec, vmem, vmem, vmem],
        out_specs=(vmem, vmem),
        scratch_shapes=[
            pltpu.VMEM((n_held, sources, chunk), jnp.bfloat16),
            pltpu.VMEM((sources // depth, depth, chunk), jnp.bfloat16),
            pltpu.VMEM((rows, sources), jnp.bfloat16),
            pltpu.VMEM((4, n_pieces, rows, piece), jnp.float32),
            pltpu.VMEM((n_pieces, rows, piece), jnp.float32),
            pltpu.VMEM((n_pieces, rows, piece), jnp.float32),
            pltpu.VMEM((2, rows, width), jnp.bfloat16),
            pltpu.VMEM((2, 8, GROUP, LANES), jnp.float32),
            pltpu.VMEM((rows, LANES), jnp.float32),
            pltpu.VMEM((rows, LANES), jnp.float32),
            dma((n_held,)), dma((sources // depth,)), dma((2,)),
            dma((n_pieces,)), dma((n_pieces,)), dma((n_pieces,)), dma((n_pieces,)),
            dma((n_pieces,)), dma((n_pieces,)), dma((n_pieces,)), dma((n_pieces,)),
            dma((8,)), dma((2, 8)),
            pltpu.SemaphoreType.REGULAR, pltpu.SemaphoreType.REGULAR,
        ],
        compiler_params=pltpu.CompilerParams(collective_id=0, has_side_effects=True, vmem_limit_bytes=67000000),
    )(a_two, emis, init_row, len_pack, len_col)


def solution(mesh):
    vec_axes = ('rows', 'states')

    def local_forward(trans_blk, emit_blk, init_blk, tokens, lengths):
        batch, n_steps = tokens.shape
        width = init_blk.shape[0]
        a_two = jnp.transpose(trans_blk, (1, 0, 2))
        flat = tokens.T.reshape(-1)
        emis = emit_blk.T.at[flat].get(mode='promise_in_bounds').reshape(n_steps, batch, width)
        len_pack = jnp.pad(lengths.reshape(batch // GROUP, GROUP).T, ((0, 0), (0, LANES - batch // GROUP)))
        len_col = jnp.broadcast_to(lengths[:, None], (batch, LANES))
        ll, alpha = run_forward(a_two, emis, init_blk[None, :], len_pack, len_col, n_steps, batch, width)
        return ll[:, :batch // GROUP].T.reshape(batch), alpha

    return jax.shard_map(local_forward, mesh=mesh, in_specs=(P('rows', None, 'states'), P(vec_axes, None), P(vec_axes), P('seqs', None), P('seqs')), out_specs=(P('seqs'), P('seqs', vec_axes)), check_vma=False)
```

time: 2870 us -> 846 us (0.29)
  waiting for transfers between devices: 1070 us -> 0 us
  matrix products: 803 us -> 0 us
  Pallas kernels: 0 us -> 745 us
  blocking collectives: 715 us -> 0 us
  other arithmetic: 139 us -> 0.01 us
    dot_general x31 -> x0, matrix products: 803 us -> none  [one_step(): jnp.einsum('bk,kaq->baq', gathered, trans_blk, preferred_element_type=jnp...]
    pallas_call x0 -> x1, Pallas kernels: none -> 745 us  [run_forward(): pl.pallas_call(functools.partial(forward_kernel, n_steps, rows, width, pi...]
    psum x32 -> x0, blocking collectives: 715 us -> none  [the longest x31 690 us: one_step(): norm_step = lax.psum(jnp.sum(raw_next, axis=1), vec_axes)]
    all_gather x31 -> x0, waiting for transfers between devices: 538 us -> none  [one_step(): lax.all_gather(alpha_cur.astype(jnp.bfloat16), 'states', axis=1, tiled=True)]
    reduce_scatter x31 -> x0, waiting for transfers between devices: 530 us -> none  [one_step(): lax.psum_scatter(part_sum, 'rows', scatter_dimension=1, tiled=True)[:, 0, :]]
    select_n x33 -> x1, other arithmetic: 55.8 us -> 0.01 us  [local_forward(): emit_blk.T.at[flat].get(mode='promise_in_bounds')]
    while x1 -> x0, local copies, waits for them, and re-layouts: 44.2 us -> none  [local_forward(): lax.scan(one_step, (alpha_init, loglik_init), (emis_all[1:], jnp.arange(1...]
    unnamed x12 -> x2, local copies, waits for them, and re-layouts: 4.01 us -> 46.1 us
  transfers between devices with their start and end apart: 62 -> 0, of which waited for: 62 -> 0; matrix products, arithmetic and copies ran while one was open for 1% -> 0% of each run, Pallas kernels for 0% -> 0%
where the time goes in v1:
time: 846 us; the launch traced here: 845 us
  Pallas kernels  745 us (88%)
  local copies, waits for them, and re-layouts  99.1 us (12%)
    pallas_call x1, Pallas kernels, run_forward(): pl.pallas_call(functools.partial(forward_kernel, n_steps, rows, width, pi...  745 us
    gather x1, local copies, waits for them, and re-layouts, local_forward(): emit_blk.T.at[flat].get(mode='promise_in_bounds')  48.1 us
    unnamed x2, local copies, waits for them, and re-layouts  46.1 us

profile of v1, /device:TPU:0, one launch (start us, length us, event | category | flops | bytes accessed | tf_op | source)
XLA Modules:
  0.0 844.7 jit_solution(11205355030270343110)
XLA Ops:
  0.6 0.7 reshape.47
  1.4 0.1 copy.8
  1.4 0.6 pad.4.len_pack
  2.0 0.8 reshape.45
  2.9 1.3 broadcast_in_dim.5.len_col
  4.2 48.1 %gather_fusion = bf16[2048,2048]{1,0:T(8,128)(2,1)} fusion(bf16[10000,2048]{1,0:T(8,128)(2,1)} %bitcast.11, s32[2048]{0:T(1024)S(1)} %broadcast_clamp_fusion), kind=kCustom, calls=%fused_computation | custom fusion | bytes 16785408 | tf_op jit(solution)/shard_map/gather | solution.py:304
  52.3 44.2 %copy.11 = bf16[8192,2,2048]{2,0,1:T(8,128)(2,1)} copy(bf16[8192,2,2048]{2,1,0:T(2,128)(2,1)} %param.5) | data formatting | bytes 134217728 | tf_op args[0]
  96.5 745.0 %shard_map.68 = (f32[8,128]{1,0:T(8,128)}, f32[64,2048]{1,0:T(8,128)}) custom-call(bf16[2,8192,2048]{2,1,0:T(8,128)(2,1)} %bitcast.10.a_hbm, bf16[32,64,2048]{2,1,0:T(8,128)(2,1)} %bitcast.12, f32[1,2048]{1,0:T(1,128)} %bitcast.16, s32[8,128]{1,0:T(8,128)} %pad.4.len_pack, s32[64,128]{1,0:T(8,128)} %broadcast_in_dim.5.len_col), custom_call_target="tpu_custom_call" | custom-call | tf_op jit(solution)/shard_map/pallas_call | solution.py:270
  841.5 0.7 slice_bitcast_fusion
  842.2 0.1 copy.9
  842.3 0.6 reshape.48
  842.9 1.9 copy.13
  (2 shorter events, 0.0 us)

commit v2 on v1

--- a/solution.py
+++ b/solution.py
@@ -14,7 +14,7 @@
 
 def forward_kernel(
     n_steps, rows, width, piece, chunk, depth,
-    a_hbm, emis_hbm, init_ref, len_pack, len_col,
+    a_hbm, emis_hbm, init_ref, end_pack, end_col,
     ll_ref, alpha_ref,
     held, ring, a_bf, gath, y_out, y_in, emis, c_buf, c_acc, inv_b,
     held_sem, ring_sem, emis_sem, y_ss, y_rs, x_ss, x_rs, p_ss, p_rs, f_ss, f_rs, c_ss, c_rs,
@@ -43,7 +43,7 @@
         pl.semaphore_signal(barrier, inc=1, device_id=peer, device_id_type=MESH)
 
     def held_copy(ch):
-        half, c = (other, ch) if ch < n_chunks else (row, ch - n_chunks)
+        half, c = (other, ch) if ch < n_chunks else (row, 2 * (ch - n_chunks) + 1)
         return pltpu.make_async_copy(a_hbm.at[half, :, pl.ds(c * chunk, chunk)], held.at[ch], held_sem.at[ch])
 
     def ring_copy(c, k):
@@ -89,7 +89,7 @@
     for ch in range(held.shape[0]):
         held_copy(ch).start()
     for k in range(k_parts):
-        ring_copy(n_held_own, k).start()
+        ring_copy(0, k).start()
     emis_copy(1, 1).start()
     pl.semaphore_wait(barrier, 7)
 
@@ -97,13 +97,15 @@
     ll_ref[...] = jnp.zeros_like(ll_ref)
     alpha_ref[...] = jnp.zeros_like(alpha_ref)
 
-    def emit_piece(p, value, cols, par):
-        r = value * emis[par, :, cols].astype(jnp.float32)
-        gath[st, p] = r
-        part = r[:, :LANES]
-        for j in range(1, piece // LANES):
-            part = part + r[:, j * LANES:(j + 1) * LANES]
-        c_acc[...] += part
+    def emit_piece(p, value, t, par):
+        for j in range(piece // LANES):
+            cols = pl.ds(pl.multiple_of(p * piece + j * LANES, LANES), LANES)
+            fresh = jnp.broadcast_to(init_ref[:, cols], (rows, LANES))
+            if value is not None:
+                fresh = jnp.where(t == end_col[0], fresh, value[:, j * LANES:(j + 1) * LANES])
+            r = fresh * emis[par, :, cols].astype(jnp.float32)
+            gath[st, p, :, j * LANES:(j + 1) * LANES] = r
+            c_acc[...] += r
         x_copy(p).start()
         p_copy(p).start()
 
@@ -128,7 +130,10 @@
         total = c_buf[par, 0]
         for k in range(1, 8):
             total = total + c_buf[par, k]
-        ll_ref[...] += jnp.where(t < len_pack[...], jnp.log(total), 0.0)
+        log_c = jnp.log(total)
+        first = t < end_pack[0]
+        ll_ref[0] += jnp.where(first, log_c, 0.0)
+        ll_ref[1] += jnp.where(jnp.logical_and(jnp.logical_not(first), t < end_pack[1]), log_c, 0.0)
         inv = 1.0 / total
         for i in range(rows // GROUP):
             inv_b[pl.ds(i * GROUP, GROUP), :] = jnp.broadcast_to(inv[:, i:i + 1], (GROUP, LANES))
@@ -166,18 +171,21 @@
             pl.semaphore_signal(credit_x, inc=1, device_id=to_x, device_id_type=MESH)
             pl.semaphore_signal(credit_p, inc=1, device_id=to_p, device_id_type=MESH)
 
-        live = t < len_col[...]
+    def capture(t):
+        first = t < end_col[0]
+        second = jnp.logical_and(jnp.logical_not(first), t < end_col[1])
         scale = inv_b[...]
         for p in range(n_pieces):
             for j in range(piece // LANES):
                 cols = pl.ds(p * piece + j * LANES, LANES)
-                alpha_ref[:, cols] = jnp.where(live, gath[st, p, :, j * LANES:(j + 1) * LANES] * scale, alpha_ref[:, cols])
+                a = gath[st, p, :, j * LANES:(j + 1) * LANES] * scale
+                alpha_ref[0, :, cols] = jnp.where(first, a, alpha_ref[0, :, cols])
+                alpha_ref[1, :, cols] = jnp.where(second, a, alpha_ref[1, :, cols])
 
     c_acc[...] = jnp.zeros_like(c_acc)
     emis_copy(0, 0).wait()
     for p in range(n_pieces):
-        cols = pl.ds(p * piece, piece)
-        emit_piece(p, jnp.broadcast_to(init_ref[:, cols], (rows, piece)), cols, 0)
+        emit_piece(p, None, 0, 0)
     finish(0, 0)
 
     def one_step(t, _):
@@ -203,6 +211,7 @@
             return 0
 
         lax.fori_loop(0, n_chunks, send_half, 0)
+        capture(t - 1)
         pl.semaphore_wait(credit_x, 1)
         pl.semaphore_wait(credit_p, 1)
         emis_copy(t, par).wait()
@@ -211,56 +220,58 @@
             for h in range(per_chunk):
                 p = c * per_chunk + h
                 y_copy(p).wait_recv()
-                cols = pl.ds(pl.multiple_of(p * piece, piece), piece)
-                emit_piece(p, out[:, h * piece:(h + 1) * piece] + y_in[p], cols, par)
-
-            @pl.when(c > 0)
-            def _():
-                for h in range(per_chunk):
-                    forward((c - 1) * per_chunk + h)
-
-        def own_held(c, _):
-            @pl.when(t == 1)
-            def _():
-                for ch in range(n_held_own):
-                    @pl.when(c == ch)
-                    def _():
-                        held_copy(n_chunks + ch).wait()
-
-            pieces(c, jnp.dot(a_bf[...], held[n_chunks + c], preferred_element_type=jnp.float32))
-            return 0
-
-        lax.fori_loop(0, n_held_own, own_held, 0)
-
-        def own_streamed(c, _):
+                emit_piece(p, out[:, h * piece:(h + 1) * piece] + y_in[p], t, par)
+
+        def forward_chunk(c):
+            for h in range(per_chunk):
+                forward(c * per_chunk + h)
+
+        def own_pair(i, _):
+            c = 2 * i
             out = None
             for k in range(k_parts):
                 ring_copy(c, k).wait()
                 term = jnp.dot(a_bf[:, k * depth:(k + 1) * depth], ring[k], preferred_element_type=jnp.float32)
                 out = term if out is None else out + term
-                last = c == n_chunks - 1
+                last = i == n_held_own - 1
 
                 @pl.when(jnp.logical_not(last))
                 def _():
-                    ring_copy(c + 1, k).start()
+                    ring_copy(c + 2, k).start()
 
                 @pl.when(jnp.logical_and(last, t < n_steps - 1))
                 def _():
-                    ring_copy(n_held_own, k).start()
+                    ring_copy(0, k).start()
 
             pieces(c, out)
+
+            @pl.when(i > 0)
+            def _():
+                forward_chunk(c - 1)
+
+            @pl.when(t == 1)
+            def _():
+                for ch in range(n_held_own):
+                    @pl.when(i == ch)
+                    def _():
+                        held_copy(n_chunks + ch).wait()
+
+            pieces(c + 1, jnp.dot(a_bf[...], held[n_chunks + i], preferred_element_type=jnp.float32))
+            forward_chunk(c)
             return 0
 
-        lax.fori_loop(n_held_own, n_chunks, own_streamed, 0)
+        lax.fori_loop(0, n_held_own, own_pair, 0)
         for p in range(n_pieces):
             y_copy(p).wait_send()
         finish(t, n_pieces - per_chunk)
         return 0
 
     lax.fori_loop(1, n_steps, one_step, 0)
-
-
-def run_forward(a_two, emis, init_row, len_pack, len_col, n_steps, rows, width):
+    capture(n_steps - 1)
+
+
+def run_forward(a_two, emis, init_row, end_pack, end_col, call_id):
+    n_steps, rows, width = emis.shape
     piece, chunk, depth, n_held = 256, 512, 2048, 6
     sources = a_two.shape[1]
     n_pieces = width // piece
@@ -269,7 +280,7 @@
     vmem = pl.BlockSpec(memory_space=pltpu.VMEM)
     return pl.pallas_call(
         functools.partial(forward_kernel, n_steps, rows, width, piece, chunk, depth),
-        out_shape=(jax.ShapeDtypeStruct((GROUP, LANES), jnp.float32), jax.ShapeDtypeStruct((rows, width), jnp.float32)),
+        out_shape=(jax.ShapeDtypeStruct((2, GROUP, LANES), jnp.float32), jax.ShapeDtypeStruct((2, rows, width), jnp.float32)),
         in_specs=[any_spec, any_spec, vmem, vmem, vmem],
         out_specs=(vmem, vmem),
         scratch_shapes=[
@@ -289,8 +300,14 @@
             dma((8,)), dma((2, 8)),
             pltpu.SemaphoreType.REGULAR, pltpu.SemaphoreType.REGULAR,
         ],
-        compiler_params=pltpu.CompilerParams(collective_id=0, has_side_effects=True, vmem_limit_bytes=67000000),
-    )(a_two, emis, init_row, len_pack, len_col)
+        compiler_params=pltpu.CompilerParams(collective_id=call_id, has_side_effects=True, vmem_limit_bytes=67000000),
+    )(a_two, emis, init_row, end_pack, end_col)
+
+
+def second_of(ranked, rows):
+    batch = ranked.shape[0]
+    alone = 2 * rows - batch
+    return jnp.concatenate([jnp.zeros((alone,) + ranked.shape[1:], ranked.dtype), ranked[rows:][::-1]])
 
 
 def solution(mesh):
@@ -300,11 +317,40 @@
         batch, n_steps = tokens.shape
         width = init_blk.shape[0]
         a_two = jnp.transpose(trans_blk, (1, 0, 2))
-        flat = tokens.T.reshape(-1)
-        emis = emit_blk.T.at[flat].get(mode='promise_in_bounds').reshape(n_steps, batch, width)
-        len_pack = jnp.pad(lengths.reshape(batch // GROUP, GROUP).T, ((0, 0), (0, LANES - batch // GROUP)))
-        len_col = jnp.broadcast_to(lengths[:, None], (batch, LANES))
-        ll, alpha = run_forward(a_two, emis, init_blk[None, :], len_pack, len_col, n_steps, batch, width)
-        return ll[:, :batch // GROUP].T.reshape(batch), alpha
+        table = emit_blk.T
+        seq = jnp.arange(batch)
+        longer = (lengths[None, :] > lengths[:, None]) | ((lengths[None, :] == lengths[:, None]) & (seq[None, :] < seq[:, None]))
+        rank = jnp.sum(longer.astype(jnp.int32), axis=1)
+        at_rank = rank[None, :] == seq[:, None]
+        len_ranked = jnp.sum(jnp.where(at_rank, lengths[None, :], 0), axis=1)
+        tok_ranked = jnp.sum(jnp.where(at_rank[:, :, None], tokens[None, :, :], 0), axis=1)
+
+        def run(rows, call_id):
+            def branch(a_two, table, init_blk, rank, len_ranked, tok_ranked):
+                end_1 = len_ranked[:rows]
+                end_2 = end_1 + second_of(len_ranked, rows)
+                step = jnp.arange(n_steps)
+                since = step[:, None] - end_1[None, :]
+                later = jnp.sum(jnp.where(since[:, :, None] == step[None, None, :], second_of(tok_ranked, rows)[None, :, :], 0), axis=2)
+                tok = jnp.where(since < 0, tok_ranked[:rows].T, later)
+                emis = table.at[tok.reshape(-1)].get(mode='promise_in_bounds').reshape(n_steps, rows, width)
+                ends = jnp.stack([end_1, end_2])
+                packed = jnp.swapaxes(ends.reshape(2, rows // GROUP, GROUP), 1, 2)
+                end_pack = jnp.pad(packed, ((0, 0), (0, 0), (0, LANES - rows // GROUP)))
+                end_col = jnp.broadcast_to(ends[:, :, None], (2, rows, LANES))
+                ll, alpha = run_forward(a_two, emis, init_blk[None, :], end_pack, end_col, call_id)
+                at = jnp.where(rank < rows, rank, 3 * rows - 1 - rank)
+                ll_rows = jnp.swapaxes(ll[:, :, :rows // GROUP], 1, 2).reshape(2 * rows)
+                loglik = jnp.sum(jnp.where(at[:, None] == jnp.arange(2 * rows)[None, :], ll_rows[None, :], 0.0), axis=1)
+                return loglik, alpha.reshape(2 * rows, width).at[at].get(mode='promise_in_bounds')
+
+            return branch
+
+        def fits(rows):
+            return jnp.max(jnp.where(jnp.arange(rows) >= 2 * rows - batch, len_ranked[:rows] + second_of(len_ranked, rows), 0)) <= n_steps
+
+        sizes = (40, 48, batch)
+        pick = jnp.where(fits(40), 0, jnp.where(fits(48), 1, 2))
+        return lax.switch(pick, [run(m, k) for k, m in enumerate(sizes)], a_two, table, init_blk, rank, len_ranked, tok_ranked)
 
     return jax.shard_map(local_forward, mesh=mesh, in_specs=(P('rows', None, 'states'), P(vec_axes, None), P(vec_axes), P('seqs', None), P('seqs')), out_specs=(P('seqs'), P('seqs', vec_axes)), check_vma=False)

time: 846 us -> 774 us (0.915)
  Pallas kernels: 745 us -> 701 us
  local copies, waits for them, and re-layouts: 99.1 us -> 65.4 us
    pallas_call x1, Pallas kernels: 745 us -> 701 us  [run_forward(): pl.pallas_call(functools.partial(forward_kernel, n_steps, rows, width, pi...]
    gather x1 -> x2, local copies, waits for them, and re-layouts: 48.1 us -> 17.6 us  [the longest x1 14.8 us: branch(): table.at[tok.reshape(-1)].get(mode='promise_in_bounds')]
    unnamed x2 -> x5, local copies, waits for them, and re-layouts: 46.1 us -> 44.2 us
where the time goes in v2:
time: 774 us
  Pallas kernels  701 us (91%)
  local copies, waits for them, and re-layouts  65.4 us (8%)
    pallas_call x1, Pallas kernels, run_forward(): pl.pallas_call(functools.partial(forward_kernel, n_steps, rows, width, pi...  701 us
    unnamed x5, local copies, waits for them, and re-layouts  44.2 us

profile of v2, /device:TPU:0, one launch (start us, length us, event | category | flops | bytes accessed | tf_op | source)
XLA Modules:
  0.0 774.0 jit_solution(9223983333117003524)
XLA Ops:
  0.6 0.9 convert_reduce_fusion
  1.5 0.8 select_reduce_fusion.8
  2.3 0.1 slice.48
  2.4 0.1 rev.19
  2.5 0.7 fusion.7
  3.9 0.1 slice.46
  3.9 0.1 rev.18
  4.0 0.7 fusion.6
  5.4 0.0 copy-start
  5.4 0.0 copy-start.1
  5.4 44.2 %copy.87 = bf16[8192,2,2048]{2,0,1:T(8,128)(2,1)} copy(bf16[8192,2,2048]{2,1,0:T(2,128)(2,1)} %param.8) | data formatting | bytes 134217728 | tf_op args[0]
  49.7 0.0 copy-done
  49.7 0.0 copy-done.1
  49.7 724.3 %conditional.1 = (f32[64]{0:T(128)}, f32[64,2048]{1,0:T(8,128)}) conditional(s32[]{:T(128)} %clamp.3, (s32[64]{0:T(128)S(1)}, s32[64]{0:T(128)S(1)}, pred[64,64]{1,0:T(8,128)(4,1)S(1)}, bf16[10000,2048]{1,0:T(8,128)(2,1)}, f32[2048]{0:T(1024)S(1)}, /*index=5*/bf16[2,8192,2048]{2,1,0:T(8,128)(2,1)}, s32[]{:T(128)}, ...), branch_computations={%region_5.8_spmd, %region_8.11_spmd, %region_11.13_spmd} | conditional | flops 438832 | bytes 18023452 | solution.py:354
  49.7 0.1 slice.33
  49.8 0.1 rev.13
  49.9 0.1 slice_bitcast_fusion.3
  50.0 0.1 iota_subtract_fusion
  50.0 0.1 copy.65
  50.1 1.2 select_reduce_fusion.2
  51.3 0.1 copy.84
  51.4 0.1 concatenate.15.clone
  51.4 0.1 select_reduce_fusion.3
  51.6 0.1 copy.67
  51.6 0.1 fusion
  51.7 0.1 copy.68
  51.8 0.1 reshape.198
  51.9 14.8 %gather_fusion.2 = bf16[1280,2048]{1,0:T(8,128)(2,1)} fusion(bf16[10000,2048]{1,0:T(8,128)(2,1)} %get-tuple-element.38, s32[2048]{0:T(1024)S(1)} %pad_clamp_fusion.1), kind=kCustom, calls=%fused_computation | custom fusion | bytes 10490880 | tf_op jit(solution)/shard_map/cond/branch_0_fun/gather | solution.py:336
  66.7 0.1 stack.14
  66.8 0.1 copy.69
  66.9 0.1 stack.20
  67.0 0.1 copy.70
  67.1 0.6 pad.15.end_pack
  67.7 0.7 broadcast_in_dim.129.end_col
  68.4 701.2 %branch_0_fun.1 = (f32[2,8,128]{2,1,0:T(8,128)}, f32[2,40,2048]{2,1,0:T(8,128)}) custom-call(bf16[2,8192,2048]{2,1,0:T(8,128)(2,1)} %get-tuple-element.37.a_hbm, bf16[32,40,2048]{2,1,0:T(8,128)(2,1)} %bitcast.50, f32[1,2048]{1,0:T(1,128)S(1)} %bitcast.52, s32[2,8,128]{2,1,0:T(8,128)} %pad.15.end_pack, s32[2,40,128]{2,1,0:T(8,128)} %broadcast_in_dim.129.end_col), custom_call_target="tpu_custom_call" | custom-call | tf_op jit(solution)/shard_map/cond/branch_0_fun/pallas_call | solution.py:281
  769.6 2.9 gather_fusion.3
  772.5 0.7 slice_bitcast_fusion.2
  773.2 0.1 copy.71
  773.2 0.1 broadcast_in_dim.130
  773.3 0.7 select_reduce_fusion.4
  (9 shorter events, 0.1 us)
Async XLA Ops:
  5.4 44.3 %copy-start = (s32[64,32]{0,1:T(8,128)S(1)}, s32[64,32]{0,1:T(8,128)}, u32[]{:S(2)}) copy-start(s32[64,32]{0,1:T(8,128)} %param.11) | copy-start | bytes 24580
  5.4 44.3 %copy-start.1 = (f32[2048]{0:T(1024)S(1)}, f32[2048]{0:T(1024)}, u32[]{:S(2)}) copy-start(f32[2048]{0:T(1024)} %param.10) | copy-start | bytes 24580

commit v3 on v2

--- a/solution.py
+++ b/solution.py
@@ -113,7 +113,7 @@
         x_arrived(p).wait_recv()
         f_copy(p).start()
 
-    def finish(t, first_forward):
+    def finish(t):
         par = lax.rem(t, 2)
         pack = jnp.zeros((GROUP, LANES), jnp.float32)
         for i in range(rows // GROUP):
@@ -123,7 +123,7 @@
         for k in range(1, 8):
             c_copy(par, k).start()
         c_acc[...] = jnp.zeros_like(c_acc)
-        for p in range(first_forward, n_pieces):
+        for p in range(n_pieces):
             forward(p)
         for k in range(1, 8):
             c_arrived(par, k).wait_recv()
@@ -186,7 +186,7 @@
     emis_copy(0, 0).wait()
     for p in range(n_pieces):
         emit_piece(p, None, 0, 0)
-    finish(0, 0)
+    finish(0)
 
     def one_step(t, _):
         par = lax.rem(t, 2)
@@ -221,10 +221,6 @@
                 p = c * per_chunk + h
                 y_copy(p).wait_recv()
                 emit_piece(p, out[:, h * piece:(h + 1) * piece] + y_in[p], t, par)
-
-        def forward_chunk(c):
-            for h in range(per_chunk):
-                forward(c * per_chunk + h)
 
         def own_pair(i, _):
             c = 2 * i
@@ -245,10 +241,6 @@
 
             pieces(c, out)
 
-            @pl.when(i > 0)
-            def _():
-                forward_chunk(c - 1)
-
             @pl.when(t == 1)
             def _():
                 for ch in range(n_held_own):
@@ -257,13 +249,12 @@
                         held_copy(n_chunks + ch).wait()
 
             pieces(c + 1, jnp.dot(a_bf[...], held[n_chunks + i], preferred_element_type=jnp.float32))
-            forward_chunk(c)
             return 0
 
         lax.fori_loop(0, n_held_own, own_pair, 0)
         for p in range(n_pieces):
             y_copy(p).wait_send()
-        finish(t, n_pieces - per_chunk)
+        finish(t)
         return 0
 
     lax.fori_loop(1, n_steps, one_step, 0)

time: 774 us -> 674 us (0.87)
  Pallas kernels: 701 us -> 601 us
    pallas_call x1, Pallas kernels: 701 us -> 601 us  [run_forward(): pl.pallas_call(functools.partial(forward_kernel, n_steps, rows, width, pi...]
where the time goes in v3:
time: 674 us; the launch traced here: 673 us
  Pallas kernels  601 us (89%)
  local copies, waits for them, and re-layouts  65.2 us (10%)
    pallas_call x1, Pallas kernels, run_forward(): pl.pallas_call(functools.partial(forward_kernel, n_steps, rows, width, pi...  601 us
    unnamed x5, local copies, waits for them, and re-layouts  44.2 us
    gather x1, local copies, waits for them, and re-layouts, branch(): table.at[tok.reshape(-1)].get(mode='promise_in_bounds')  14.6 us

profile of v3, /device:TPU:0, one launch (start us, length us, event | category | flops | bytes accessed | tf_op | source)
XLA Modules:
  0.0 673.4 jit_solution(5765148080528113233)
XLA Ops:
  0.6 0.9 convert_reduce_fusion
  1.5 0.8 select_reduce_fusion.8
  2.3 0.1 slice.48
  2.4 0.1 rev.19
  2.5 0.7 fusion.7
  3.9 0.1 slice.46
  3.9 0.1 rev.18
  4.0 0.7 fusion.6
  5.4 0.0 copy-start
  5.4 0.0 copy-start.1
  5.4 44.2 %copy.87 = bf16[8192,2,2048]{2,0,1:T(8,128)(2,1)} copy(bf16[8192,2,2048]{2,1,0:T(2,128)(2,1)} %param.8) | data formatting | bytes 134217728 | tf_op args[0]
  49.7 0.0 copy-done
  49.7 0.0 copy-done.1
  49.7 623.7 %conditional.1 = (f32[64]{0:T(128)}, f32[64,2048]{1,0:T(8,128)}) conditional(s32[]{:T(128)} %clamp.3, (s32[64]{0:T(128)S(1)}, s32[64]{0:T(128)S(1)}, pred[64,64]{1,0:T(8,128)(4,1)S(1)}, bf16[10000,2048]{1,0:T(8,128)(2,1)}, f32[2048]{0:T(1024)S(1)}, /*index=5*/bf16[2,8192,2048]{2,1,0:T(8,128)(2,1)}, s32[]{:T(128)}, ...), branch_computations={%region_5.8_spmd, %region_8.11_spmd, %region_11.13_spmd} | conditional | flops 438832 | bytes 18023452 | solution.py:345
  49.7 0.1 slice.33
  49.8 0.1 rev.13
  49.9 0.1 slice_bitcast_fusion.3
  50.0 0.1 iota_subtract_fusion
  50.0 0.1 copy.65
  50.1 1.2 select_reduce_fusion.2
  51.3 0.1 copy.84
  51.4 0.1 concatenate.15.clone
  51.4 0.1 select_reduce_fusion.3
  51.6 0.1 copy.67
  51.6 0.1 fusion
  51.7 0.1 copy.68
  51.8 0.1 reshape.198
  51.9 14.6 %gather_fusion.2 = bf16[1280,2048]{1,0:T(8,128)(2,1)} fusion(bf16[10000,2048]{1,0:T(8,128)(2,1)} %get-tuple-element.38, s32[2048]{0:T(1024)S(1)} %pad_clamp_fusion.1), kind=kCustom, calls=%fused_computation | custom fusion | bytes 10490880 | tf_op jit(solution)/shard_map/cond/branch_0_fun/gather | solution.py:327
  66.5 0.1 stack.14
  66.6 0.1 copy.69
  66.7 0.1 stack.20
  66.8 0.1 copy.70
  66.9 0.6 pad.15.end_pack
  67.5 0.7 broadcast_in_dim.129.end_col
  68.2 600.7 %branch_0_fun.1 = (f32[2,8,128]{2,1,0:T(8,128)}, f32[2,40,2048]{2,1,0:T(8,128)}) custom-call(bf16[2,8192,2048]{2,1,0:T(8,128)(2,1)} %get-tuple-element.37.a_hbm, bf16[32,40,2048]{2,1,0:T(8,128)(2,1)} %bitcast.50, f32[1,2048]{1,0:T(1,128)S(1)} %bitcast.52, s32[2,8,128]{2,1,0:T(8,128)} %pad.15.end_pack, s32[2,40,128]{2,1,0:T(8,128)} %broadcast_in_dim.129.end_col), custom_call_target="tpu_custom_call" | custom-call | tf_op jit(solution)/shard_map/cond/branch_0_fun/pallas_call | solution.py:272
  669.0 2.9 gather_fusion.3
  671.8 0.7 slice_bitcast_fusion.2
  672.5 0.1 copy.71
  672.6 0.1 broadcast_in_dim.130
  672.7 0.7 select_reduce_fusion.4
  (9 shorter events, 0.1 us)
Async XLA Ops:
  5.4 44.3 %copy-start = (s32[64,32]{0,1:T(8,128)S(1)}, s32[64,32]{0,1:T(8,128)}, u32[]{:S(2)}) copy-start(s32[64,32]{0,1:T(8,128)} %param.11) | copy-start | bytes 24580
  5.4 44.3 %copy-start.1 = (f32[2048]{0:T(1024)S(1)}, f32[2048]{0:T(1024)}, u32[]{:S(2)}) copy-start(f32[2048]{0:T(1024)} %param.10) | copy-start | bytes 24580

commit v4 on v3

--- a/solution.py
+++ b/solution.py
@@ -59,14 +59,17 @@
     def y_copy(p):
         return remote(y_out.at[p], y_in.at[p], y_ss.at[p], y_rs.at[p], to_y)
 
-    def x_copy(p):
-        return remote(gath.at[st, p], gath.at[st, p], x_ss.at[p], x_rs.at[p], to_x)
+    def own_slot(par):
+        return st + par * (4 - st)
+
+    def x_copy(p, par):
+        return remote(gath.at[own_slot(par), p], gath.at[st, p], x_ss.at[p], x_rs.at[p], to_x)
 
     def x_arrived(p):
         return remote(gath.at[across, p], gath.at[across, p], x_ss.at[p], x_rs.at[p], to_x)
 
-    def p_copy(p):
-        return remote(gath.at[st, p], gath.at[st, p], p_ss.at[p], p_rs.at[p], to_p)
+    def p_copy(p, par):
+        return remote(gath.at[own_slot(par), p], gath.at[st, p], p_ss.at[p], p_rs.at[p], to_p)
 
     def p_arrived(p):
         return remote(gath.at[partner, p], gath.at[partner, p], p_ss.at[p], p_rs.at[p], to_p)
@@ -104,14 +107,26 @@
             if value is not None:
                 fresh = jnp.where(t == end_col[0], fresh, value[:, j * LANES:(j + 1) * LANES])
             r = fresh * emis[par, :, cols].astype(jnp.float32)
-            gath[st, p, :, j * LANES:(j + 1) * LANES] = r
+            gath[own_slot(par), p, :, j * LANES:(j + 1) * LANES] = r
             c_acc[...] += r
-        x_copy(p).start()
-        p_copy(p).start()
+        x_copy(p, par).start()
+        p_copy(p, par).start()
 
     def forward(p):
         x_arrived(p).wait_recv()
         f_copy(p).start()
+
+    def capture(t):
+        first = t < end_col[0]
+        second = jnp.logical_and(jnp.logical_not(first), t < end_col[1])
+        scale = inv_b[...]
+        for p in range(n_pieces):
+            for j in range(piece // LANES):
+                cols = pl.ds(p * piece + j * LANES, LANES)
+                a = gath[own_slot(lax.rem(t, 2)), p, :, j * LANES:(j + 1) * LANES] * scale
+                alpha_ref[0, :, cols] = jnp.where(first, a, alpha_ref[0, :, cols])
+                if alpha_ref.shape[0] > 1:
+                    alpha_ref[1, :, cols] = jnp.where(second, a, alpha_ref[1, :, cols])
 
     def finish(t):
         par = lax.rem(t, 2)
@@ -123,6 +138,8 @@
         for k in range(1, 8):
             c_copy(par, k).start()
         c_acc[...] = jnp.zeros_like(c_acc)
+        if not isinstance(t, int):
+            capture(t - 1)
         for p in range(n_pieces):
             forward(p)
         for k in range(1, 8):
@@ -138,15 +155,15 @@
         for i in range(rows // GROUP):
             inv_b[pl.ds(i * GROUP, GROUP), :] = jnp.broadcast_to(inv[:, i:i + 1], (GROUP, LANES))
 
-        def convert(src, p):
+        def convert(slot, src, p):
             scale = inv_b[...]
             for j in range(piece // LANES):
                 at = pl.multiple_of(src * width + p * piece + j * LANES, LANES)
-                a_bf[:, pl.ds(at, LANES)] = (gath[src, p, :, j * LANES:(j + 1) * LANES] * scale).astype(jnp.bfloat16)
+                a_bf[0:rows, pl.ds(at, LANES)] = (gath[slot, p, :, j * LANES:(j + 1) * LANES] * scale).astype(jnp.bfloat16)
 
         def convert_own(p, _):
-            convert(st, p)
-            convert(across, p)
+            convert(own_slot(par), st, p)
+            convert(across, across, p)
             return 0
 
         lax.fori_loop(0, n_pieces, convert_own, 0)
@@ -154,14 +171,15 @@
         def convert_near(p, _):
             p_arrived(p).wait_recv()
             f_arrived(p).wait_recv()
-            convert(partner, p)
-            convert(lax.rem(partner + 2, 4), p)
+            convert(partner, partner, p)
+            far = lax.rem(partner + 2, 4)
+            convert(far, far, p)
             return 0
 
         lax.fori_loop(0, n_pieces, convert_near, 0)
         for p in range(n_pieces):
-            x_copy(p).wait_send()
-            p_copy(p).wait_send()
+            x_copy(p, par).wait_send()
+            p_copy(p, par).wait_send()
             f_copy(p).wait_send()
         for k in range(1, 8):
             c_copy(par, k).wait_send()
@@ -171,17 +189,8 @@
             pl.semaphore_signal(credit_x, inc=1, device_id=to_x, device_id_type=MESH)
             pl.semaphore_signal(credit_p, inc=1, device_id=to_p, device_id_type=MESH)
 
-    def capture(t):
-        first = t < end_col[0]
-        second = jnp.logical_and(jnp.logical_not(first), t < end_col[1])
-        scale = inv_b[...]
-        for p in range(n_pieces):
-            for j in range(piece // LANES):
-                cols = pl.ds(p * piece + j * LANES, LANES)
-                a = gath[st, p, :, j * LANES:(j + 1) * LANES] * scale
-                alpha_ref[0, :, cols] = jnp.where(first, a, alpha_ref[0, :, cols])
-                alpha_ref[1, :, cols] = jnp.where(second, a, alpha_ref[1, :, cols])
-
+    if a_bf.shape[0] > rows:
+        a_bf[rows:, :] = jnp.zeros((a_bf.shape[0] - rows, a_bf.shape[1]), jnp.bfloat16)
     c_acc[...] = jnp.zeros_like(c_acc)
     emis_copy(0, 0).wait()
     for p in range(n_pieces):
@@ -203,15 +212,14 @@
                     def _():
                         held_copy(ch).wait()
 
-            out = jnp.dot(a_bf[...], held[c], preferred_element_type=jnp.float32)
+            out = jnp.dot(a_bf[...], held[c], preferred_element_type=jnp.float32)[0:rows]
             for h in range(per_chunk):
                 p = c * per_chunk + h
                 y_out[p] = out[:, h * piece:(h + 1) * piece]
                 y_copy(p).start()
             return 0
 
-        lax.fori_loop(0, n_chunks, send_half, 0)
-        capture(t - 1)
+        lax.fori_loop(0, n_held_own, send_half, 0)
         pl.semaphore_wait(credit_x, 1)
         pl.semaphore_wait(credit_p, 1)
         emis_copy(t, par).wait()
@@ -224,10 +232,11 @@
 
         def own_pair(i, _):
             c = 2 * i
+            lax.fori_loop(2 + 2 * i, 3 + i, send_half, 0)
             out = None
             for k in range(k_parts):
                 ring_copy(c, k).wait()
-                term = jnp.dot(a_bf[:, k * depth:(k + 1) * depth], ring[k], preferred_element_type=jnp.float32)
+                term = jnp.dot(a_bf[:, k * depth:(k + 1) * depth], ring[k], preferred_element_type=jnp.float32)[0:rows]
                 out = term if out is None else out + term
                 last = i == n_held_own - 1
 
@@ -240,6 +249,7 @@
                     ring_copy(0, k).start()
 
             pieces(c, out)
+            lax.fori_loop(3 + i, n_chunks, send_half, 0)
 
             @pl.when(t == 1)
             def _():
@@ -248,7 +258,7 @@
                     def _():
                         held_copy(n_chunks + ch).wait()
 
-            pieces(c + 1, jnp.dot(a_bf[...], held[n_chunks + i], preferred_element_type=jnp.float32))
+            pieces(c + 1, jnp.dot(a_bf[...], held[n_chunks + i], preferred_element_type=jnp.float32)[0:rows])
             return 0
 
         lax.fori_loop(0, n_held_own, own_pair, 0)
@@ -261,7 +271,7 @@
     capture(n_steps - 1)
 
 
-def run_forward(a_two, emis, init_row, end_pack, end_col, call_id):
+def run_forward(a_two, emis, init_row, end_pack, end_col, n_seqs, call_id):
     n_steps, rows, width = emis.shape
     piece, chunk, depth, n_held = 256, 512, 2048, 6
     sources = a_two.shape[1]
@@ -271,14 +281,14 @@
     vmem = pl.BlockSpec(memory_space=pltpu.VMEM)
     return pl.pallas_call(
         functools.partial(forward_kernel, n_steps, rows, width, piece, chunk, depth),
-        out_shape=(jax.ShapeDtypeStruct((2, GROUP, LANES), jnp.float32), jax.ShapeDtypeStruct((2, rows, width), jnp.float32)),
+        out_shape=(jax.ShapeDtypeStruct((2, GROUP, LANES), jnp.float32), jax.ShapeDtypeStruct((n_seqs, rows, width), jnp.float32)),
         in_specs=[any_spec, any_spec, vmem, vmem, vmem],
         out_specs=(vmem, vmem),
         scratch_shapes=[
             pltpu.VMEM((n_held, sources, chunk), jnp.bfloat16),
             pltpu.VMEM((sources // depth, depth, chunk), jnp.bfloat16),
-            pltpu.VMEM((rows, sources), jnp.bfloat16),
-            pltpu.VMEM((4, n_pieces, rows, piece), jnp.float32),
+            pltpu.VMEM((128 if rows <= 48 else rows, sources), jnp.bfloat16),
+            pltpu.VMEM((5, n_pieces, rows, piece), jnp.float32),
             pltpu.VMEM((n_pieces, rows, piece), jnp.float32),
             pltpu.VMEM((n_pieces, rows, piece), jnp.float32),
             pltpu.VMEM((2, rows, width), jnp.bfloat16),
@@ -329,11 +339,11 @@
                 packed = jnp.swapaxes(ends.reshape(2, rows // GROUP, GROUP), 1, 2)
                 end_pack = jnp.pad(packed, ((0, 0), (0, 0), (0, LANES - rows // GROUP)))
                 end_col = jnp.broadcast_to(ends[:, :, None], (2, rows, LANES))
-                ll, alpha = run_forward(a_two, emis, init_blk[None, :], end_pack, end_col, call_id)
+                ll, alpha = run_forward(a_two, emis, init_blk[None, :], end_pack, end_col, 2 if rows < batch else 1, call_id)
                 at = jnp.where(rank < rows, rank, 3 * rows - 1 - rank)
                 ll_rows = jnp.swapaxes(ll[:, :, :rows // GROUP], 1, 2).reshape(2 * rows)
                 loglik = jnp.sum(jnp.where(at[:, None] == jnp.arange(2 * rows)[None, :], ll_rows[None, :], 0.0), axis=1)
-                return loglik, alpha.reshape(2 * rows, width).at[at].get(mode='promise_in_bounds')
+                return loglik, alpha.reshape(-1, width).at[at].get(mode='promise_in_bounds')
 
             return branch
 

time: 674 us -> 624 us (0.926)
  Pallas kernels: 601 us -> 550 us
    pallas_call x1, Pallas kernels: 601 us -> 550 us  [run_forward(): pl.pallas_call(functools.partial(forward_kernel, n_steps, rows, width, pi...]
where the time goes in v4:
time: 624 us
  Pallas kernels  550 us (88%)
  local copies, waits for them, and re-layouts  65.7 us (11%)
    pallas_call x1, Pallas kernels, run_forward(): pl.pallas_call(functools.partial(forward_kernel, n_steps, rows, width, pi...  550 us
    unnamed x5, local copies, waits for them, and re-layouts  44.2 us
    gather x1, local copies, waits for them, and re-layouts, branch(): table.at[tok.reshape(-1)].get(mode='promise_in_bounds')  15.1 us

profile of v4, /device:TPU:0, one launch (start us, length us, event | category | flops | bytes accessed | tf_op | source)
XLA Modules:
  0.0 623.6 jit_solution(10728936610741729647)
XLA Ops:
  0.6 0.9 convert_reduce_fusion
  1.5 0.8 select_reduce_fusion.8
  2.3 0.1 slice.48
  2.4 0.1 rev.19
  2.5 0.7 fusion.7
  3.9 0.1 slice.46
  3.9 0.1 rev.18
  4.0 0.7 fusion.6
  5.4 0.0 copy-start
  5.4 0.0 copy-start.1
  5.4 44.2 %copy.87 = bf16[8192,2,2048]{2,0,1:T(8,128)(2,1)} copy(bf16[8192,2,2048]{2,1,0:T(2,128)(2,1)} %param.8) | data formatting | bytes 134217728 | tf_op args[0]
  49.7 0.0 copy-done
  49.7 0.0 copy-done.1
  49.7 573.9 %conditional.1 = (f32[64]{0:T(128)}, f32[64,2048]{1,0:T(8,128)}) conditional(s32[]{:T(128)} %clamp.3, (s32[64]{0:T(128)S(1)}, s32[64]{0:T(128)S(1)}, pred[64,64]{1,0:T(8,128)(4,1)S(1)}, bf16[10000,2048]{1,0:T(8,128)(2,1)}, f32[2048]{0:T(1024)S(1)}, /*index=5*/bf16[2,8192,2048]{2,1,0:T(8,128)(2,1)}, s32[]{:T(128)}, ...), branch_computations={%region_5.8_spmd, %region_8.11_spmd, %region_11.13_spmd} | conditional | flops 438832 | bytes 18023452 | solution.py:355
  49.7 0.1 slice.33
  49.8 0.1 rev.13
  49.9 0.1 slice_bitcast_fusion.3
  50.0 0.1 iota_subtract_fusion
  50.0 0.1 copy.65
  50.1 1.2 select_reduce_fusion.2
  51.3 0.1 copy.84
  51.4 0.1 concatenate.15.clone
  51.4 0.1 select_reduce_fusion.3
  51.6 0.1 copy.67
  51.6 0.1 fusion
  51.7 0.1 copy.68
  51.8 0.1 reshape.198
  51.9 15.1 %gather_fusion.2 = bf16[1280,2048]{1,0:T(8,128)(2,1)} fusion(bf16[10000,2048]{1,0:T(8,128)(2,1)} %get-tuple-element.38, s32[2048]{0:T(1024)S(1)} %pad_clamp_fusion.1), kind=kCustom, calls=%fused_computation | custom fusion | bytes 10490880 | tf_op jit(solution)/shard_map/cond/branch_0_fun/gather | solution.py:337
  67.1 0.1 stack.14
  67.1 0.1 copy.69
  67.2 0.1 stack.20
  67.3 0.1 copy.70
  67.4 0.6 pad.15.end_pack
  68.0 0.7 broadcast_in_dim.129.end_col
  68.7 550.4 %branch_0_fun.1 = (f32[2,8,128]{2,1,0:T(8,128)}, f32[2,40,2048]{2,1,0:T(8,128)}) custom-call(bf16[2,8192,2048]{2,1,0:T(8,128)(2,1)} %get-tuple-element.37.a_hbm, bf16[32,40,2048]{2,1,0:T(8,128)(2,1)} %bitcast.51, f32[1,2048]{1,0:T(1,128)S(1)} %bitcast.52, s32[2,8,128]{2,1,0:T(8,128)} %pad.15.end_pack, s32[2,40,128]{2,1,0:T(8,128)} %broadcast_in_dim.129.end_col), custom_call_target="tpu_custom_call" | custom-call | tf_op jit(solution)/shard_map/cond/branch_0_fun/pallas_call | solution.py:282
  619.2 2.9 gather_fusion.3
  622.0 0.7 slice_bitcast_fusion.2
  622.7 0.1 copy.71
  622.8 0.1 broadcast_in_dim.130
  622.9 0.7 select_reduce_fusion.4
  (9 shorter events, 0.1 us)
Async XLA Ops:
  5.4 44.3 %copy-start = (s32[64,32]{0,1:T(8,128)S(1)}, s32[64,32]{0,1:T(8,128)}, u32[]{:S(2)}) copy-start(s32[64,32]{0,1:T(8,128)} %param.11) | copy-start | bytes 24580
  5.4 44.3 %copy-start.1 = (f32[2048]{0:T(1024)S(1)}, f32[2048]{0:T(1024)}, u32[]{:S(2)}) copy-start(f32[2048]{0:T(1024)} %param.10) | copy-start | bytes 24580

commit v5 on v4

--- a/solution.py
+++ b/solution.py
@@ -89,10 +89,8 @@
         return remote(c_buf.at[par, src], c_buf.at[par, src], c_ss.at[k], c_rs.at[par, k], peers[k - 1])
 
     emis_copy(0, 0).start()
-    for ch in range(held.shape[0]):
+    for ch in range(n_chunks - 2):
         held_copy(ch).start()
-    for k in range(k_parts):
-        ring_copy(0, k).start()
     emis_copy(1, 1).start()
     pl.semaphore_wait(barrier, 7)
 
@@ -195,7 +193,12 @@
     emis_copy(0, 0).wait()
     for p in range(n_pieces):
         emit_piece(p, None, 0, 0)
+    held_copy(n_chunks - 2).start()
+    for k in range(k_parts):
+        ring_copy(0, k).start()
     finish(0)
+    for ch in range(n_chunks - 1, held.shape[0]):
+        held_copy(ch).start()
 
     def one_step(t, _):
         par = lax.rem(t, 2)

time: 624 us -> 616 us (0.987)
  Pallas kernels: 550 us -> 542 us
    pallas_call x1, Pallas kernels: 550 us -> 542 us  [run_forward(): pl.pallas_call(functools.partial(forward_kernel, n_steps, rows, width, pi...]
where the time goes in v5:
time: 616 us; the launch traced here: 615 us
  Pallas kernels  542 us (88%)
  local copies, waits for them, and re-layouts  65.5 us (11%)
    pallas_call x1, Pallas kernels, run_forward(): pl.pallas_call(functools.partial(forward_kernel, n_steps, rows, width, pi...  542 us
    unnamed x5, local copies, waits for them, and re-layouts  44.2 us
    gather x1, local copies, waits for them, and re-layouts, branch(): table.at[tok.reshape(-1)].get(mode='promise_in_bounds')  14.9 us

profile of v5, /device:TPU:0, one launch (start us, length us, event | category | flops | bytes accessed | tf_op | source)
XLA Modules:
  0.0 615.2 jit_solution(14800195676448072052)
XLA Ops:
  0.6 0.9 convert_reduce_fusion
  1.5 0.8 select_reduce_fusion.8
  2.3 0.1 slice.48
  2.4 0.1 rev.19
  2.5 0.7 fusion.7
  3.9 0.1 slice.46
  3.9 0.1 rev.18
  4.0 0.7 fusion.6
  5.4 0.0 copy-start
  5.4 0.0 copy-start.1
  5.4 44.2 %copy.87 = bf16[8192,2,2048]{2,0,1:T(8,128)(2,1)} copy(bf16[8192,2,2048]{2,1,0:T(2,128)(2,1)} %param.8) | data formatting | bytes 134217728 | tf_op args[0]
  49.7 0.0 copy-done
  49.7 0.0 copy-done.1
  49.7 565.5 %conditional.1 = (f32[64]{0:T(128)}, f32[64,2048]{1,0:T(8,128)}) conditional(s32[]{:T(128)} %clamp.3, (s32[64]{0:T(128)S(1)}, s32[64]{0:T(128)S(1)}, pred[64,64]{1,0:T(8,128)(4,1)S(1)}, bf16[10000,2048]{1,0:T(8,128)(2,1)}, f32[2048]{0:T(1024)S(1)}, /*index=5*/bf16[2,8192,2048]{2,1,0:T(8,128)(2,1)}, s32[]{:T(128)}, ...), branch_computations={%region_5.8_spmd, %region_8.11_spmd, %region_11.13_spmd} | conditional | flops 438832 | bytes 18023452 | solution.py:358
  49.7 0.1 slice.33
  49.8 0.1 rev.13
  49.9 0.1 slice_bitcast_fusion.3
  50.0 0.1 iota_subtract_fusion
  50.0 0.1 copy.65
  50.1 1.2 select_reduce_fusion.2
  51.3 0.1 copy.84
  51.4 0.1 concatenate.15.clone
  51.4 0.1 select_reduce_fusion.3
  51.6 0.1 copy.67
  51.6 0.1 fusion
  51.7 0.1 copy.68
  51.8 0.1 reshape.198
  51.9 14.9 %gather_fusion.2 = bf16[1280,2048]{1,0:T(8,128)(2,1)} fusion(bf16[10000,2048]{1,0:T(8,128)(2,1)} %get-tuple-element.38, s32[2048]{0:T(1024)S(1)} %pad_clamp_fusion.1), kind=kCustom, calls=%fused_computation | custom fusion | bytes 10490880 | tf_op jit(solution)/shard_map/cond/branch_0_fun/gather | solution.py:340
  66.8 0.1 stack.14
  66.9 0.1 copy.69
  67.0 0.1 stack.20
  67.1 0.1 copy.70
  67.2 0.6 pad.15.end_pack
  67.8 0.7 broadcast_in_dim.129.end_col
  68.5 542.3 %branch_0_fun.1 = (f32[2,8,128]{2,1,0:T(8,128)}, f32[2,40,2048]{2,1,0:T(8,128)}) custom-call(bf16[2,8192,2048]{2,1,0:T(8,128)(2,1)} %get-tuple-element.37.a_hbm, bf16[32,40,2048]{2,1,0:T(8,128)(2,1)} %bitcast.51, f32[1,2048]{1,0:T(1,128)S(1)} %bitcast.52, s32[2,8,128]{2,1,0:T(8,128)} %pad.15.end_pack, s32[2,40,128]{2,1,0:T(8,128)} %broadcast_in_dim.129.end_col), custom_call_target="tpu_custom_call" | custom-call | tf_op jit(solution)/shard_map/cond/branch_0_fun/pallas_call | solution.py:285
  610.8 2.9 gather_fusion.3
  613.6 0.7 slice_bitcast_fusion.2
  614.3 0.1 copy.71
  614.4 0.1 broadcast_in_dim.130
  614.5 0.7 select_reduce_fusion.4
  (9 shorter events, 0.1 us)
Async XLA Ops:
  5.4 44.3 %copy-start = (s32[64,32]{0,1:T(8,128)S(1)}, s32[64,32]{0,1:T(8,128)}, u32[]{:S(2)}) copy-start(s32[64,32]{0,1:T(8,128)} %param.11) | copy-start | bytes 24580
  5.4 44.3 %copy-start.1 = (f32[2048]{0:T(1024)S(1)}, f32[2048]{0:T(1024)}, u32[]{:S(2)}) copy-start(f32[2048]{0:T(1024)} %param.10) | copy-start | bytes 24580
